TPU v7x, 256 devices: a whole 4x4x8 slice. The times are simulated.
256 devices in a mesh: row: 8 (over z), col: 32 (over y, x, core).
Axes of the slice: x: 4, y: 4, z: 8, core: 2. Of those that a mesh axis runs over, the one named last changes fastest.
Arguments:
- front_matrix: bfloat16 [32768, 32768], P('row', 'col'), may hold values from -0.03125 to 0.03125
- right_random: bfloat16 [32768, 128], P(('col', 'row')), may hold values from -32 to 32
- left_random: bfloat16 [32768, 128], P(('row', 'col')), may hold values from -32 to 32
- row_basis: bfloat16 [32768, 384], P('row'), may hold values from -1 to 1, as said below
- column_basis: bfloat16 [32768, 384], P('col'), may hold values from -1 to 1, as said below
Outputs:
- row_samples: float32 [128, 32768], P('col', 'row')
- column_samples: float32 [128, 32768], P('row', 'col')
- row_spread: float32 [64], P('row')
- column_spread: float32 [64], P('col')
Inputs may be any that keep to these rules, and one draw needn't show every extreme that they name: Within each leaf node's 512 rows, the columns of row_basis are orthonormal up to their rounding to bfloat16. Within each leaf node's 512 rows, the columns of column_basis are orthonormal up to their rounding to bfloat16.
All inputs are finite; a program needn't handle non-finite values.
Results may differ from a plain program's by a relative error of at most 0.0003.
Values may be sent and summed in bfloat16 or wider, within the bound.
A program may use at most 64 MiB of HBM per device.

v0:
```python
import jax
import jax.numpy as jnp
from jax import lax
from jax.sharding import Mesh
from jax.sharding import PartitionSpec as P

SAMPLES = 128
EARLIER = 384
NODE = 512
COL = ("col_0", "col_1", "col_2")
COL_ROW = ("col_0", "col_1", "col_2", "row")
ROW_COL = ("row", "col_0", "col_1", "col_2")


def copy_for_each(value, axis):
    copies = jnp.broadcast_to(value, (lax.axis_size(axis), *value.shape))
    return lax.all_to_all(copies, axis, split_axis=0, concat_axis=0, tiled=True)


def joined_along(pieces, dim):
    pieces = jnp.moveaxis(pieces, 0, dim)
    shape = pieces.shape
    return pieces.reshape(*shape[:dim], shape[dim] * shape[dim + 1], *shape[dim + 2 :])


def gathered_copies(value, axis, dim):
    pieces = copy_for_each(value, axis)
    return joined_along(pieces, dim)


def in_blocks(value, dim, length):
    before, after = (value.shape[:dim], value.shape[dim + 1 :])
    return jnp.moveaxis(value.reshape(*before, length, -1, *after), dim, 0)


def summed_on_arrival(value, axis, dim):
    pieces = in_blocks(value, dim, lax.axis_size(axis))
    arrived = lax.all_to_all(pieces, axis, split_axis=0, concat_axis=0, tiled=True)
    return arrived.sum(axis=0)


def one_axis_at_a_time(value, axes):
    for axis in axes:
        value = lax.psum(value, axis)
    return value


def project_out(samples, basis):
    count = samples.shape[0]
    nodes = basis.shape[0] // NODE
    shaped = samples.reshape(count, nodes, NODE)
    stacked = basis.astype(jnp.float32).reshape(nodes, NODE, EARLIER)
    coeffs = jnp.einsum("knr,nre->kne", shaped, stacked, precision=lax.Precision.HIGHEST)
    correction = jnp.einsum("kne,nre->knr", coeffs, stacked, precision=lax.Precision.HIGHEST)
    cleaned = shaped - correction
    squares = jnp.sum(cleaned * cleaned, axis=(0, 2))
    return (cleaned.reshape(count, nodes * NODE), squares)


def shards(front_matrix, right_random, left_random, row_basis, column_basis):
    row_partial = jnp.einsum(
        "jc,ij->ci",
        gathered_copies(right_random, "row", 0),
        front_matrix,
        preferred_element_type=jnp.float32,
    )
    column_partial = jnp.einsum(
        "ic,ij->cj",
        gathered_copies(left_random, COL, 0),
        front_matrix,
        preferred_element_type=jnp.float32,
    )
    row_mine = summed_on_arrival(row_partial, COL, 0)
    column_mine = summed_on_arrival(column_partial, "row", 0)
    row_samples, row_partial_sq = project_out(row_mine, row_basis)
    column_samples, column_partial_sq = project_out(column_mine, column_basis)
    row_total_sq = one_axis_at_a_time(row_partial_sq, COL)
    column_total_sq = lax.psum(column_partial_sq, "row")
    row_spread = jnp.sqrt(row_total_sq / (SAMPLES * NODE))
    column_spread = jnp.sqrt(column_total_sq / (SAMPLES * NODE))
    return (row_samples, column_samples, row_spread, column_spread)


def solution(mesh):
    split = Mesh(
        mesh.devices.reshape(mesh.shape["row"], 4, 4, 2), ("row", "col_0", "col_1", "col_2")
    )
    placed = (P("row", COL), P(COL_ROW, None), P(ROW_COL, None), P("row", None), P(COL, None))
    return jax.shard_map(
        shards,
        mesh=split,
        in_specs=placed,
        out_specs=(P(COL, "row"), P("row", COL), P("row"), P(COL)),
        check_vma=False,
    )
```

profile of v0, /device:TPU:1, one launch (start us, length us, event | category | flops | bytes accessed | tf_op | source)
XLA Modules:
  0.0 134.8 jit_solution(16208003830906486168)
XLA Ops:
  0.6 0.0 copy-start
  0.6 0.0 copy-start.1
  0.7 1.0 copy.27
  1.7 1.3 broadcast_in_dim.7
  3.0 8.6 %all-to-all-start.2 = ((bf16[32,128,128]{1,2,0:T(8,128)(2,1)}), bf16[32,128,128]{1,2,0:T(8,128)(2,1)}, u32[]{:S(2)}, u32[]{:S(2)}) async-start(bf16[32,128,128]{1,2,0:T(8,128)(2,1)} %broadcast_in_dim.7), calls=%async_computation.2 | async-start | bytes 2097152 | tf_op jit(solution)/shard_map/all_to_all | solution.py:17
  11.6 0.0 copy-done.1
  11.6 0.1 copy.22
  11.7 17.0 %all-to-all-done.2 = bf16[32,128,128]{1,2,0:T(8,128)(2,1)} async-done(((bf16[32,128,128]{1,2,0:T(8,128)(2,1)}), bf16[32,128,128]{1,2,0:T(8,128)(2,1)}, u32[]{:S(2)}, u32[]{:S(2)}) %all-to-all-start.2) | async-done | bytes 1048608 | tf_op jit(solution)/shard_map/all_to_all | solution.py:17
  28.7 0.7 broadcast_in_dim.6
  29.4 8.2 %all-to-all-start = ((bf16[8,128,128]{1,2,0:T(8,128)(2,1)}), bf16[8,128,128]{1,2,0:T(8,128)(2,1)S(1)}, u32[]{:S(2)}, u32[]{:S(2)}) async-start(bf16[8,128,128]{1,2,0:T(8,128)(2,1)} %broadcast_in_dim.6), calls=%async_computation | async-start | bytes 524288 | tf_op jit(solution)/shard_map/all_to_all | solution.py:17
  37.6 2.3 %copy.28 = bf16[32,128,128]{2,1,0:T(8,128)(2,1)} copy(bf16[32,128,128]{1,2,0:T(8,128)(2,1)} %all-to-all-done.2) | data formatting | bytes 2097152 | tf_op jit(solution)/shard_map/all_to_all | solution.py:17
  39.9 2.3 %copy.29 = bf16[128,4096]{1,0:T(8,128)(2,1)} copy(bf16[128,4096]{0,1:T(8,128)(2,1)} %bitcast.46) | data formatting | bytes 2097152 | tf_op jit(solution)/shard_map/ic,ij->cj/dot_general | solution.py:67
  42.2 5.8 %fusion = f32[8,16,1024]{2,1,0:T(8,128)} fusion(bf16[8,16,4096]{2,1,0:T(8,128)(2,1)} %bitcast.45, bf16[4096,1024]{1,0:T(8,128)(2,1)} %param.5), kind=kOutput, calls=%fused_computation | convolution fusion | flops 1073741824 | bytes 9961472 | tf_op jit(solution)/shard_map/ic,ij->cj/dot_general | solution.py:67
  47.9 0.7 all-to-all-done
  48.6 5.9 %all-to-all-start.3 = ((f32[8,16,1024]{2,1,0:T(8,128)}), f32[8,16,1024]{2,1,0:T(8,128)}, u32[]{:S(2)}, u32[]{:S(2)}) async-start(f32[8,16,1024]{2,1,0:T(8,128)} %fusion), calls=%async_computation.3 | async-start | bytes 1048576 | tf_op jit(solution)/shard_map/all_to_all | solution.py:38
  54.6 0.8 copy.23
  55.4 1.1 copy.24
  56.5 0.8 dot_general.27
  57.3 6.4 %fusion.2 = f32[32,4,4096]{2,0,1:T(8,128)S(1)} fusion(bf16[4096,1024]{1,0:T(8,128)(2,1)} %param.5, bf16[32,4,1024]{2,1,0:T(4,128)(2,1)} %dot_general.27), kind=kOutput, calls=%fused_computation.2 | convolution fusion | flops 1073741824 | bytes 10747904 | tf_op jit(solution)/shard_map/jc,ij->ci/dot_general | solution.py:61
  63.7 2.7 %copy.26 = f32[32,4,4096]{2,1,0:T(4,128)} copy(f32[32,4,4096]{2,0,1:T(8,128)S(1)} %fusion.2) | data formatting | bytes 4194304 | tf_op jit(solution)/shard_map/jc,ij->ci/dot_general | solution.py:61
  66.4 5.3 %all-to-all-done.3 = f32[8,16,1024]{2,1,0:T(8,128)} async-done(((f32[8,16,1024]{2,1,0:T(8,128)}), f32[8,16,1024]{2,1,0:T(8,128)}, u32[]{:S(2)}, u32[]{:S(2)}) %all-to-all-start.3) | async-done | bytes 524320 | tf_op jit(solution)/shard_map/all_to_all | solution.py:38
  71.7 5.8 %all-to-all-start.1 = ((f32[32,4,4096]{2,1,0:T(4,128)}), f32[32,4,4096]{2,1,0:T(4,128)}, u32[]{:S(2)}, u32[]{:S(2)}) async-start(f32[32,4,4096]{2,1,0:T(4,128)} %copy.26), calls=%async_computation.1 | async-start | bytes 4194304 | tf_op jit(solution)/shard_map/all_to_all | solution.py:38
  77.5 1.1 reduce_sum.37
  78.6 1.5 %convolution_bitcast_fusion.2 = f32[16,2,384]{2,0,1:T(8,128)S(1)} fusion(bf16[2,512,384]{2,1,0:T(8,128)(2,1)} %bitcast.47, f32[2,2,8,512]{3,2,1,0:T(8,128)S(1)} %bitcast.52), kind=kOutput, calls=%fused_computation.8 | convolution fusion | flops 75497472 | bytes 901120 | tf_op jit(solution)/shard_map/knr,nre->kne/dot_general | solution.py:53
  80.1 2.0 %multiply_reduce_fusion = (f32[2]{0:T(128)S(1)}, f32[16,2,512]{2,0,1:T(8,128)S(1)}) fusion(f32[16,2,384]{2,0,1:T(8,128)S(1)} %convolution_bitcast_fusion.2, bf16[2,512,384]{2,1,0:T(8,128)(2,1)} %bitcast.48, f32[2,2,8,512]{3,2,1,0:T(8,128)S(1)} %bitcast.53), kind=kOutput, calls=%fused_computation.12 | convolution fusion | flops 75546624 | bytes 966664 | tf_op jit(solution)/shard_map/kne,nre->knr/dot_general | solution.py:54
  82.1 12.5 %psum.31 = f32[2]{0:T(128)S(1)} all-reduce(f32[2]{0:T(128)S(1)} %get-tuple-element.6), channel_id=1, replica_groups=mesh['row'=8,'col_0'=4,'col_1'=4,'col_2'=2] {'row'}, use_global_device_ids=true, to_apply=%region_7.0 | all-reduce | flops 2 | bytes 16 | tf_op jit(solution)/shard_map/psum | solution.py:78
  94.6 11.2 %all-to-all-done.1 = f32[32,4,4096]{2,1,0:T(4,128)} async-done(((f32[32,4,4096]{2,1,0:T(4,128)}), f32[32,4,4096]{2,1,0:T(4,128)}, u32[]{:S(2)}, u32[]{:S(2)}) %all-to-all-start.1) | async-done | bytes 2097184 | tf_op jit(solution)/shard_map/all_to_all | solution.py:38
  105.9 1.9 %reduce_sum.36 = f32[4,4096]{1,0:T(4,128)S(1)} reduce(f32[32,4,4096]{2,1,0:T(4,128)} %all-to-all-done.1, f32[]{:T(128)} %constant.2.clone.1), dimensions={0}, to_apply=%region_0.0 | reduce | flops 507904 | bytes 2162692 | tf_op jit(solution)/shard_map/reduce_sum | solution.py:39
  107.8 0.0 copy-done
  107.8 1.3 convolution_bitcast_fusion.3
  109.1 3.2 %multiply_reduce_fusion.1 = (f32[8]{0:T(128)S(1)}, f32[4,8,512]{2,0,1:T(4,128)}) fusion(f32[4,8,512]{2,0,1:T(4,128)S(1)} %bitcast.51, f32[4,8,384]{2,0,1:T(4,128)S(1)} %convolution_bitcast_fusion.3, bf16[8,512,384]{2,1,0:T(8,128)(2,1)S(1)} %bitcast.44), kind=kOutput, calls=%fused_computation.13 | convolution fusion | flops 75546616 | bytes 3325984 | tf_op jit(solution)/shard_map/kne,nre->knr/dot_general | solution.py:54
  112.3 6.3 %psum.28 = f32[8]{0:T(128)S(1)} all-reduce(f32[8]{0:T(128)S(1)} %get-tuple-element.4), channel_id=1, replica_groups=mesh['row'=8,'col_0'=4,'col_1'=4,'col_2'=2] {'col_0'}, use_global_device_ids=true, to_apply=%region_3.0 | all-reduce | flops 8 | bytes 64 | tf_op jit(solution)/shard_map/psum | solution.py:44
  118.6 0.5 multiply_sqrt_fusion
  119.1 9.2 %psum.29 = f32[8]{0:T(128)S(1)} all-reduce(f32[8]{0:T(128)S(1)} %psum.28), channel_id=1, replica_groups=mesh['row'=8,'col_0'=4,'col_1'=4,'col_2'=2] {'col_1'}, use_global_device_ids=true, to_apply=%region_4.0 | all-reduce | flops 8 | bytes 64 | tf_op jit(solution)/shard_map/psum | solution.py:44
  128.4 0.6 copy.34
  129.0 5.2 %psum.30 = f32[8]{0:T(128)S(1)} all-reduce(f32[8]{0:T(128)S(1)} %psum.29), channel_id=1, replica_groups=mesh['row'=8,'col_0'=4,'col_1'=4,'col_2'=2] {'col_2'}, use_global_device_ids=true, to_apply=%region_5.0 | all-reduce | flops 8 | bytes 64 | tf_op jit(solution)/shard_map/psum | solution.py:44
  134.2 0.5 multiply_sqrt_fusion.1
Async XLA Ops:
  0.6 107.1 %copy-start = (bf16[4096,384]{1,0:T(8,128)(2,1)S(1)}, bf16[4096,384]{1,0:T(8,128)(2,1)}, u32[]{:S(2)}) copy-start(bf16[4096,384]{1,0:T(8,128)(2,1)} %param.8) | copy-start | bytes 9437188
  0.6 11.0 %copy-start.1 = (bf16[128,128]{1,0:T(8,128)(2,1)S(1)}, bf16[128,128]{1,0:T(8,128)(2,1)}, u32[]{:S(2)}) copy-start(bf16[128,128]{1,0:T(8,128)(2,1)} %param.6) | copy-start | bytes 98308
  3.0 25.7 %all-to-all-start.2 = ((bf16[32,128,128]{1,2,0:T(8,128)(2,1)}), bf16[32,128,128]{1,2,0:T(8,128)(2,1)}, u32[]{:S(2)}, u32[]{:S(2)}) async-start(bf16[32,128,128]{1,2,0:T(8,128)(2,1)} %broadcast_in_dim.7), calls=%async_computation.2 | async-start | bytes 2097152 | tf_op jit(solution)/shard_map/all_to_all | solution.py:17
  29.4 19.2 %all-to-all-start = ((bf16[8,128,128]{1,2,0:T(8,128)(2,1)}), bf16[8,128,128]{1,2,0:T(8,128)(2,1)S(1)}, u32[]{:S(2)}, u32[]{:S(2)}) async-start(bf16[8,128,128]{1,2,0:T(8,128)(2,1)} %broadcast_in_dim.6), calls=%async_computation | async-start | bytes 524288 | tf_op jit(solution)/shard_map/all_to_all | solution.py:17
  48.6 23.1 %all-to-all-start.3 = ((f32[8,16,1024]{2,1,0:T(8,128)}), f32[8,16,1024]{2,1,0:T(8,128)}, u32[]{:S(2)}, u32[]{:S(2)}) async-start(f32[8,16,1024]{2,1,0:T(8,128)} %fusion), calls=%async_computation.3 | async-start | bytes 1048576 | tf_op jit(solution)/shard_map/all_to_all | solution.py:38
  71.7 34.1 %all-to-all-start.1 = ((f32[32,4,4096]{2,1,0:T(4,128)}), f32[32,4,4096]{2,1,0:T(4,128)}, u32[]{:S(2)}, u32[]{:S(2)}) async-start(f32[32,4,4096]{2,1,0:T(4,128)} %copy.26), calls=%async_computation.1 | async-start | bytes 4194304 | tf_op jit(solution)/shard_map/all_to_all | solution.py:38
where the time goes:
time: 136 us; the launch traced here: 135 us
  waiting for transfers between devices  34.2 us (25%)
  blocking collectives  33.3 us (24%)
  starting transfers between devices  28.5 us (21%)
  matrix products  20.1 us (15%)
  local copies, waits for them, and re-layouts  13.8 us (10%)
  other arithmetic  4.03 us (3%)
    psum x3, blocking collectives, one_axis_at_a_time(): value = lax.psum(value, axis)  20.8 us
    all_to_all x2, waiting for transfers between devices, copy_for_each(): return lax.all_to_all(copies, axis, split_axis=0, concat_axis=0, tiled=True)  17.7 us
    all_to_all x2, starting transfers between devices, copy_for_each(): return lax.all_to_all(copies, axis, split_axis=0, concat_axis=0, tiled=True)  16.8 us
    all_to_all x2, waiting for transfers between devices, summed_on_arrival(): lax.all_to_all(pieces, axis, split_axis=0, concat_axis=0, tiled=True)  16.6 us
    psum x1, blocking collectives, shards(): column_total_sq = lax.psum(column_partial_sq, 'row')  12.5 us
    all_to_all x2, starting transfers between devices, summed_on_arrival(): lax.all_to_all(pieces, axis, split_axis=0, concat_axis=0, tiled=True)  11.7 us
    dot_general x1, matrix products, shards(): jnp.einsum('jc,ij->ci', gathered_copies(right_random, 'row', 0), front_ma...  6.35 us
    dot_general x1, matrix products, shards(): jnp.einsum('ic,ij->cj', gathered_copies(left_random, COL, 0), front_matri...  5.77 us
  transfers between devices with their start and end apart: 4, of which 4 were waited for; matrix products, arithmetic and copies ran while one was open for 20% of the time, Pallas kernels for 0%

commit v1 on v0

v1 whole, which is shorter than its diff:
```python
import functools

import jax
import jax.numpy as jnp
from jax import lax
from jax.experimental import pallas as pl
from jax.experimental.pallas import tpu as pltpu
from jax.sharding import PartitionSpec as P

F32 = jnp.float32
BF16 = jnp.bfloat16
MESH = pl.DeviceIdType.MESH
NODE = 512
EARLIER = 384
SAMPLES = 128
NZ = 8
ROWS = 4096
COLS = 1024
QS = 4


def three_parts(value):
    hi = value.astype(BF16).astype(F32)
    rest = value - hi
    mid = rest.astype(BF16).astype(F32)
    low = rest - mid
    return jnp.concatenate([hi, mid, low], axis=0).astype(BF16)


def joined(stacked, count):
    return stacked[:count] + stacked[count : 2 * count] + stacked[2 * count :]


def coeffs_of(value, basis):
    out = lax.dot_general(
        three_parts(value), basis, (((1,), (0,)), ((), ())), preferred_element_type=F32
    )
    return joined(out, value.shape[0])


def correction_of(coeffs, basis):
    out = lax.dot_general(
        three_parts(coeffs), basis, (((1,), (1,)), ((), ())), preferred_element_type=F32
    )
    return joined(out, coeffs.shape[0])


def kernel(
    a_hbm, r_hbm, l_hbm, rb_hbm, cb_hbm,
    row_out, col_out, rs_out, cs_out,
    a_v, rg, l_raw, lg, rb_v, cb_v, rowacc, cacc, cr, sx, srecv,
    ra_aug, ra_fin, rb_aug, rb_fin, vrow, vrow_all, vcol, vcol_all,
    in_sem, a_sem,
    r_ss, r_rs, la_ss, la_rs, lb_ss, lb_rs, lp_ss, lp_rs,
    d_ss, d_rs, sa_ss, sa_rs, sb_ss, sb_rs, c_ss, c_rs,
    vr_ss, vr_rs, vc_ss, vc_rs,
):
    z = lax.axis_index("row")
    c = lax.axis_index("col")
    core = lax.rem(c, 2)
    other = 1 - core
    x = lax.rem(lax.div(c, 2), 4)
    y = lax.div(c, 8)
    a0 = core * y + other * x
    b0 = core * x + other * y
    stride_a = 2 + 6 * core
    stride_b = 8 - 6 * core

    def za(step):
        return lax.rem(z + step + NZ, NZ)

    def at_a(step):
        return lax.rem(a0 + step + 4, 4)

    def at_b(step):
        return lax.rem(b0 + step + 4, 4)

    def dev_a(step):
        return (z, at_a(step) * stride_a + b0 * stride_b + core)

    def dev_b(step):
        return (z, a0 * stride_a + at_b(step) * stride_b + core)

    def dev_z(step):
        return (za(step), c)

    partner = (z, c + 1 - 2 * core)

    def remote(src, dst, ssem, rsem, device):
        return pltpu.make_async_remote_copy(
            src_ref=src, dst_ref=dst, send_sem=ssem, recv_sem=rsem,
            device_id=device, device_id_type=MESH,
        )

    sent = []

    def send(copy):
        copy.start()
        sent.append(copy)

    r_in = pltpu.make_async_copy(r_hbm, rg.at[z], in_sem.at[0])
    l_in = pltpu.make_async_copy(l_hbm, l_raw, in_sem.at[1])
    r_in.start()
    l_in.start()
    a_in = []
    for part in range(8):
        rows = pl.ds(part * NODE, NODE)
        copy = pltpu.make_async_copy(a_hbm.at[rows], a_v.at[rows], a_sem.at[part])
        copy.start()
        a_in.append(copy)
    rb_in = pltpu.make_async_copy(rb_hbm, rb_v, in_sem.at[2])
    cb_in = pltpu.make_async_copy(cb_hbm, cb_v, in_sem.at[3])
    cb_in.start()
    rb_in.start()

    barrier = pltpu.get_barrier_semaphore()
    peers = [dev_z(1), dev_z(-1), dev_a(1), dev_a(-1), dev_b(1), dev_b(-1), partner]
    for peer in peers:
        pl.semaphore_signal(barrier, inc=1, device_id=peer, device_id_type=MESH)
    l_in.wait()
    own_u = a0 * 4 + b0
    lg[core, own_u] = l_raw[...].T
    r_in.wait()
    pl.semaphore_wait(barrier, len(peers))

    def r_copy(side, step):
        d = 1 if side == 0 else -1
        block = za(-d * (step - 1))
        if step < 4:
            ref = rg.at[block]
        else:
            ref = rg.at[block, pl.ds(64 * side, 64)]
        return remote(ref, ref, r_ss.at[side, step - 1], r_rs.at[side, step - 1], dev_z(d))

    def r_forward(step):
        for side in (0, 1):
            r_copy(side, step).wait_recv()
            if step < 4:
                send(r_copy(side, step + 1))

    def l_slot(ra, rb):
        return at_a(ra) * 4 + at_b(rb)

    def la_full(side):
        d = 1 if side == 0 else -1
        ref = lg.at[core, own_u]
        return remote(ref, ref, la_ss.at[0, side], la_rs.at[0, side], dev_a(d))

    def la_half(side):
        d = 1 if side == 0 else -1
        ref = lg.at[core, l_slot(-d, 0), pl.ds(64 * side, 64)]
        return remote(ref, ref, la_ss.at[1, side], la_rs.at[1, side], dev_a(d))

    def lb_full(ra, side):
        d = 1 if side == 0 else -1
        ref = lg.at[core, l_slot(ra, 0)]
        return remote(ref, ref, lb_ss.at[0, ra, side], lb_rs.at[0, ra, side], dev_b(d))

    def lb_half(ra, side):
        d = 1 if side == 0 else -1
        ref = lg.at[core, l_slot(ra, -d), pl.ds(64 * side, 64)]
        return remote(ref, ref, lb_ss.at[1, ra, side], lb_rs.at[1, ra, side], dev_b(d))

    def lp(ra, rb):
        ref = lg.at[core, l_slot(ra, rb)]
        return remote(ref, ref, lp_ss.at[ra, rb], lp_rs.at[ra, rb], partner)

    def lb_arrived(ra):
        for side in (0, 1):
            lb_full(ra, side).wait_recv()
            send(lb_half(ra, side))
        for side in (0, 1):
            send(lp(ra, 3 if side == 0 else 1))

    def lb_two_arrived(ra):
        for side in (0, 1):
            lb_half(ra, side).wait_recv()
        send(lp(ra, 2))

    def row_term(rows, one, two, weights):
        left = jnp.concatenate(
            [
                a_v[rows, pl.ds(pl.multiple_of(one * 128, 128), 128)],
                a_v[rows, pl.ds(pl.multiple_of(two * 128, 128), 128)],
            ],
            axis=1,
        )
        return jnp.dot(left, weights, preferred_element_type=F32)

    def r_pair(one, two):
        return jnp.concatenate([rg[one], rg[two]], axis=0)

    def row_pass(one, two, first):
        weights = r_pair(one, two)

        def body(part, carry):
            rows = pl.ds(pl.multiple_of(part * NODE, NODE), NODE)
            term = row_term(rows, one, two, weights)
            if first:
                rowacc[rows, :] = term
            else:
                rowacc[rows, :] += term
            return carry

        lax.fori_loop(0, 8, body, 0)

    def col_pass(mine, rb, first):
        if mine:
            cc, sa, sb, b_at = core, stride_a, stride_b, at_b(rb)
        else:
            cc, sa, sb = other, 2 + 6 * other, 8 - 6 * other
            b_at = lax.rem(a0 + rb, 4)
        left = jnp.concatenate([lg[cc, a * 4 + b_at] for a in range(4)], axis=1)
        starts = [pl.multiple_of((a * sa + b_at * sb + cc) * 128, 128) for a in range(4)]

        def body(part, carry):
            lanes = pl.ds(pl.multiple_of(part * 256, 256), 256)
            right = jnp.concatenate([a_v[pl.ds(s, 128), lanes] for s in starts], axis=0)
            term = jnp.dot(left, right, preferred_element_type=F32).reshape(NZ, 2, 8, 256)
            if first:
                cacc[:, :, :, lanes] = term
            else:
                cacc[:, :, :, lanes] += term
            return carry

        lax.fori_loop(0, 4, body, 0)

    for side in (0, 1):
        send(r_copy(side, 1))
    for side in (0, 1):
        send(la_full(side))
        send(lb_full(0, side))
    send(lp(0, 0))

    r_forward(1)
    for side in (0, 1):
        la_full(side).wait_recv()
        send(la_half(side))
        ra = 3 if side == 0 else 1
        send(lb_full(ra, 0))
        send(lb_full(ra, 1))
    send(lp(3, 0))
    send(lp(1, 0))
    lb_arrived(0)
    for copy in a_in:
        copy.wait()
    row_pass(za(1), za(-1), True)

    r_forward(2)
    for side in (0, 1):
        la_half(side).wait_recv()
    send(lb_full(2, 0))
    send(lb_full(2, 1))
    send(lp(2, 0))
    lb_arrived(1)
    lb_arrived(3)
    lb_two_arrived(0)
    row_pass(za(2), za(-2), False)
    col_pass(True, 0, True)

    r_forward(3)
    lb_arrived(2)
    lb_two_arrived(1)
    lb_two_arrived(3)
    row_pass(za(3), za(-3), False)
    col_pass(True, 1, False)
    col_pass(True, 3, False)
    for ra in range(4):
        lp(ra, 0).wait_recv()
    col_pass(False, 0, False)

    lb_two_arrived(2)
    r_forward(4)

    weights = r_pair(z, za(4))
    sub = lax.broadcasted_iota(jnp.int32, (16, 8, NODE), 1)

    def d_copy(q):
        return remote(sx.at[other, q], srecv.at[q], d_ss.at[q], d_rs.at[q], partner)

    for q in range(QS):
        halves = []
        for h in (0, 1):
            rows = pl.ds((q + 4 * h) * NODE, NODE)
            total = rowacc[rows, :] + row_term(rows, z, za(4), weights)
            halves.append(total.T.reshape(16, 8, NODE))
        low, high = halves
        to0 = jnp.where(sub < 4, low, pltpu.roll(high, 4, 1))
        to1 = jnp.where(sub < 4, pltpu.roll(low, 4, 1), high)
        for t in range(16):
            ty, tx = t // 4, t % 4
            sx[0, q, tx * 4 + ty] = to0[t]
            sx[1, q, ty * 4 + tx] = to1[t]
        send(d_copy(q))

    for rb in (1, 3):
        for ra in range(4):
            lp(ra, rb).wait_recv()
        col_pass(False, rb, False)
    col_pass(True, 2, False)
    for ra in range(4):
        lp(ra, 2).wait_recv()
    col_pass(False, 2, False)

    def hops(side, h):
        return 4 if side == h else 3

    def c_copy(side, reach, h, n):
        d = 1 if side == 0 else -1
        return remote(
            cacc.at[za(d * reach), h, :, pl.ds(n * NODE, NODE)],
            cr.at[side, reach - 1, h, n],
            c_ss.at[side, reach - 1, h, n],
            c_rs.at[side, reach - 1, h, n],
            dev_z(d),
        )

    def c_step(step):
        for h_first in (True, False):
            for n in (0, 1):
                for side in (0, 1):
                    h = side if h_first else 1 - side
                    reach = hops(side, h) - step + 1
                    if reach < 2:
                        continue
                    d = 1 if side == 0 else -1
                    c_copy(side, reach, h, n).wait_recv()
                    lanes = pl.ds(n * NODE, NODE)
                    cacc[za(d * (reach - 1)), h, :, lanes] += cr[side, reach - 1, h, n]
                    send(c_copy(side, reach - 1, h, n))

    for h_first in (True, False):
        for n in (0, 1):
            for side in (0, 1):
                h = side if h_first else 1 - side
                send(c_copy(side, hops(side, h), h, n))

    def sa_copy(kind, q, side):
        d = 1 if side == 0 else -1
        if kind == 0:
            src = sx.at[core, q, pl.ds(at_a(2) * 4 + 2 * side, 2)]
            dst = ra_aug.at[side, q]
        else:
            half = 1 - side if kind == 1 else side
            src = sx.at[core, q, pl.ds(at_a(d) * 4 + 2 * half, 2)]
            dst = ra_fin.at[side, q, half]
        return remote(src, dst, sa_ss.at[kind, q, side], sa_rs.at[kind, q, side], dev_a(d))

    def sb_copy(kind, q, side):
        d = 1 if side == 0 else -1
        if kind == 0:
            src = sx.at[core, q, a0 * 4 + at_b(2), :, pl.ds(256 * side, 256)]
            dst = rb_aug.at[side, q]
        else:
            half = 1 - side if kind == 1 else side
            src = sx.at[core, q, a0 * 4 + at_b(d), :, pl.ds(256 * half, 256)]
            dst = rb_fin.at[side, q, half]
        return remote(src, dst, sb_ss.at[kind, q, side], sb_rs.at[kind, q, side], dev_b(d))

    for q in range(QS):
        d_copy(q).wait_recv()
        sx[core, q] += srecv[q]
        for kind in (0, 1):
            for side in (0, 1):
                send(sa_copy(kind, q, side))
    c_step(1)
    for q in range(QS):
        for side in (0, 1):
            d = 1 if side == 0 else -1
            sa_copy(0, q, side).wait_recv()
            sx[core, q, pl.ds(at_a(d) * 4 + 2 * side, 2)] += ra_aug[side, q]
            send(sa_copy(2, q, side))
    c_step(2)
    for q in range(QS):
        for kind in (1, 2):
            for side in (0, 1):
                sa_copy(kind, q, side).wait_recv()
        for half in (0, 1):
            sx[core, q, pl.ds(a0 * 4 + 2 * half, 2)] += ra_fin[0, q, half] + ra_fin[1, q, half]
        for kind in (0, 1):
            for side in (0, 1):
                send(sb_copy(kind, q, side))
    c_step(3)
    for q in range(QS):
        for side in (0, 1):
            d = 1 if side == 0 else -1
            sb_copy(0, q, side).wait_recv()
            sx[core, q, a0 * 4 + at_b(d), :, pl.ds(256 * side, 256)] += rb_aug[side, q]
            send(sb_copy(2, q, side))

    lane8 = lax.broadcasted_iota(jnp.int32, (8, 128), 1)
    sub8 = lax.broadcasted_iota(jnp.int32, (8, 128), 0)
    cb_in.wait()
    col_sq = jnp.zeros((8, 128), F32)
    for n in (0, 1):
        lanes = pl.ds(n * NODE, NODE)
        parts = []
        for h in (0, 1):
            for side in (0, 1):
                c_copy(side, 1, h, n).wait_recv()
            parts.append(cacc[z, h, :, lanes] + cr[0, 0, h, n] + cr[1, 0, h, n])
        full = jnp.concatenate(parts, axis=0)
        basis = cb_v[pl.ds(n * NODE, NODE), :]
        cleaned = full - correction_of(coeffs_of(full, basis), basis)
        col_out[:, lanes] = cleaned
        sq = jnp.sum(cleaned * cleaned, axis=1, keepdims=True)
        col_sq = col_sq + jnp.where(lane8 == n, sq[:8] + sq[8:], 0.0)
    vcol[...] = col_sq

    def vc_copy(j):
        return remote(vcol, vcol_all.at[j], vc_ss.at[j], vc_rs.at[j], dev_z(j))

    def vr_copy(j):
        return remote(
            vrow, vrow_all.at[j], vr_ss.at[j], vr_rs.at[j], (z, lax.rem(c + j, 32))
        )

    def loop(first, last, what):
        def body(j, carry):
            what(j)
            return carry

        lax.fori_loop(first, last, body, 0)

    loop(1, NZ, lambda j: vc_copy(j).start())

    rb_in.wait()
    row_sq = jnp.zeros((8, 128), F32)
    sub_n = lax.broadcasted_iota(jnp.int32, (8, EARLIER), 0)
    sub_r = lax.broadcasted_iota(jnp.int32, (8, NODE), 0)
    for q in range(QS):
        for kind in (1, 2):
            for side in (0, 1):
                sb_copy(kind, q, side).wait_recv()
        full = sx[core, q, own_u] + jnp.concatenate(
            [rb_fin[0, q, h] + rb_fin[1, q, h] for h in (0, 1)], axis=1
        )
        low_basis = rb_v[pl.ds(q * NODE, NODE), :]
        high_basis = rb_v[pl.ds((q + 4) * NODE, NODE), :]
        coeffs = jnp.where(
            sub_n < 4, coeffs_of(full, low_basis), coeffs_of(full, high_basis)
        )
        correction = jnp.where(
            sub_r < 4, correction_of(coeffs, low_basis), correction_of(coeffs, high_basis)
        )
        cleaned = full - correction
        row_out[:, pl.ds(q * NODE, NODE)] = cleaned[:4]
        row_out[:, pl.ds((q + 4) * NODE, NODE)] = cleaned[4:]
        sq = jnp.sum(cleaned * cleaned, axis=1, keepdims=True)
        place = jnp.where(sub8 < 4, q, q + 4)
        row_sq = row_sq + jnp.where(lane8 == place, sq, 0.0)
    vrow[...] = row_sq
    loop(1, 32, lambda j: vr_copy(j).start())

    loop(1, NZ, lambda j: vc_copy(j).wait_recv())
    col_total = vcol[...]
    for j in range(1, NZ):
        col_total = col_total + vcol_all[j]
    scale = 1.0 / (SAMPLES * NODE)
    col_lane = jnp.sum(col_total, axis=0, keepdims=True)
    cs_out[...] = jnp.sqrt(col_lane * scale)[:, :2]

    for copy in sent:
        copy.wait_send()
    loop(1, NZ, lambda j: vc_copy(j).wait_send())

    loop(1, 32, lambda j: vr_copy(j).wait_recv())
    row_total = vrow[...]
    for j in range(1, 32):
        row_total = row_total + vrow_all[j]
    row_lane = jnp.sum(row_total, axis=0, keepdims=True)
    rs_out[...] = jnp.sqrt(row_lane * scale)[:, :8]
    loop(1, 32, lambda j: vr_copy(j).wait_send())


def shards(front_matrix, right_random, left_random, row_basis, column_basis):
    vmem = pltpu.VMEM
    dma = pltpu.SemaphoreType.DMA
    row, col, rs, cs = pl.pallas_call(
        kernel,
        out_shape=(
            jax.ShapeDtypeStruct((4, ROWS), F32),
            jax.ShapeDtypeStruct((16, COLS), F32),
            jax.ShapeDtypeStruct((1, 8), F32),
            jax.ShapeDtypeStruct((1, 2), F32),
        ),
        in_specs=[pl.BlockSpec(memory_space=pl.ANY)] * 5,
        out_specs=[pl.BlockSpec(memory_space=pltpu.VMEM)] * 4,
        scratch_shapes=[
            vmem((ROWS, COLS), BF16),
            vmem((NZ, 128, 128), BF16),
            vmem((128, 128), BF16),
            vmem((2, 16, 128, 128), BF16),
            vmem((ROWS, EARLIER), BF16),
            vmem((COLS, EARLIER), BF16),
            vmem((ROWS, 128), F32),
            vmem((NZ, 2, 8, COLS), F32),
            vmem((2, 4, 2, 2, 8, NODE), F32),
            vmem((2, QS, 16, 8, NODE), F32),
            vmem((QS, 16, 8, NODE), F32),
            vmem((2, QS, 2, 8, NODE), F32),
            vmem((2, QS, 2, 2, 8, NODE), F32),
            vmem((2, QS, 8, 256), F32),
            vmem((2, QS, 2, 8, 256), F32),
            vmem((8, 128), F32),
            vmem((32, 8, 128), F32),
            vmem((8, 128), F32),
            vmem((NZ, 8, 128), F32),
            dma((4,)), dma((8,)),
            dma((2, 4)), dma((2, 4)),
            dma((2, 2)), dma((2, 2)),
            dma((2, 4, 2)), dma((2, 4, 2)),
            dma((4, 4)), dma((4, 4)),
            dma((QS,)), dma((QS,)),
            dma((3, QS, 2)), dma((3, QS, 2)),
            dma((3, QS, 2)), dma((3, QS, 2)),
            dma((2, 4, 2, 2)), dma((2, 4, 2, 2)),
            dma((32,)), dma((32,)),
            dma((NZ,)), dma((NZ,)),
        ],
        compiler_params=pltpu.CompilerParams(
            collective_id=0, has_side_effects=True, vmem_limit_bytes=48 * 1024 * 1024
        ),
        name="hss_sample",
    )(front_matrix, right_random, left_random, row_basis, column_basis)
    return row, col, rs.reshape(8), cs.reshape(2)


def solution(mesh):
    return jax.shard_map(
        shards,
        mesh=mesh,
        in_specs=(
            P("row", "col"), P(("col", "row"), None), P(("row", "col"), None),
            P("row", None), P("col", None),
        ),
        out_specs=(P("col", "row"), P("row", "col"), P("row"), P("col")),
        check_vma=False,
    )
```

time: 136 us -> 61.7 us (0.45)
  Pallas kernels: 0 us -> 54 us
  waiting for transfers between devices: 34.2 us -> 0 us
  blocking collectives: 33.3 us -> 0 us
  starting transfers between devices: 28.5 us -> 0 us
  matrix products: 20.1 us -> 0 us
  local copies, waits for them, and re-layouts: 13.8 us -> 6.81 us
  other arithmetic: 4.03 us -> 0 us
    pallas_call x0 -> x1, Pallas kernels: none -> 54 us  [shards(): pl.pallas_call(kernel, out_shape=(jax.ShapeDtypeStruct((4, ROWS), F32), j...]
    all_to_all x4 -> x0, waiting for transfers between devices: 34.2 us -> none  [the longest x2 17.7 us: copy_for_each(): return lax.all_to_all(copies, axis, split_axis=0, concat_axis=0, tiled=True)]
    psum x4 -> x0, blocking collectives: 33.3 us -> none  [the longest x3 20.8 us: one_axis_at_a_time(): value = lax.psum(value, axis)]
    all_to_all x4 -> x0, starting transfers between devices: 28.5 us -> none  [the longest x2 16.8 us: copy_for_each(): return lax.all_to_all(copies, axis, split_axis=0, concat_axis=0, tiled=True)]
    dot_general x6 -> x0, matrix products: 20.1 us -> none  [the longest x1 6.35 us: shards(): jnp.einsum('jc,ij->ci', gathered_copies(right_random, 'row', 0), front_ma...]
    dot_general x4 -> x0, local copies, waits for them, and re-layouts: 6.85 us -> none  [the longest x3 4.59 us: shards(): jnp.einsum('jc,ij->ci', gathered_copies(right_random, 'row', 0), front_ma...]
    unnamed x6 -> x12, local copies, waits for them, and re-layouts: 1.14 us -> 6.81 us
    all_to_all x2 -> x0, local copies, waits for them, and re-layouts: 3.13 us -> none  [copy_for_each(): return lax.all_to_all(copies, axis, split_axis=0, concat_axis=0, tiled=True)]
  transfers between devices with their start and end apart: 4 -> 0, of which waited for: 4 -> 0; matrix products, arithmetic and copies ran while one was open for 20% -> 0% of each run, Pallas kernels for 0% -> 0%
where the time goes in v1:
time: 61.7 us; the launch traced here: 61.4 us
  Pallas kernels  54 us (88%)
  local copies, waits for them, and re-layouts  6.81 us (11%)
  between operations  0.65 us (1%)
    pallas_call x1, Pallas kernels, shards(): pl.pallas_call(kernel, out_shape=(jax.ShapeDtypeStruct((4, ROWS), F32), j...  54 us
    unnamed x12, local copies, waits for them, and re-layouts  6.81 us

profile of v1, /device:TPU:1, one launch (start us, length us, event | category | flops | bytes accessed | tf_op | source)
XLA Modules:
  0.0 61.4 jit_solution(2639683107814624681)
XLA Ops:
  0.6 0.0 copy-start
  0.6 1.9 %copy-done = bf16[4096,384]{1,0:T(8,128)(2,1)S(1)} copy-done((bf16[4096,384]{1,0:T(8,128)(2,1)S(1)}, bf16[4096,384]{1,0:T(8,128)(2,1)}, u32[]{:S(2)}) %copy-start) | copy-done | bytes 3145752
  2.5 0.0 copy-start.1
  2.5 1.1 %copy-done.1 = bf16[1024,384]{1,0:T(8,128)(2,1)S(1)} copy-done((bf16[1024,384]{1,0:T(8,128)(2,1)S(1)}, bf16[1024,384]{1,0:T(8,128)(2,1)}, u32[]{:S(2)}) %copy-start.1) | copy-done | bytes 786456
  3.7 0.0 copy-start.2
  3.7 0.8 %copy-done.2 = bf16[128,128]{1,0:T(8,128)(2,1)S(1)} copy-done((bf16[128,128]{1,0:T(8,128)(2,1)S(1)}, bf16[128,128]{1,0:T(8,128)(2,1)}, u32[]{:S(2)}) %copy-start.2) | copy-done | bytes 32792
  4.4 0.0 copy-start.3
  4.4 0.8 %copy-done.3 = bf16[128,128]{1,0:T(8,128)(2,1)S(1)} copy-done((bf16[128,128]{1,0:T(8,128)(2,1)S(1)}, bf16[128,128]{1,0:T(8,128)(2,1)}, u32[]{:S(2)}) %copy-start.3) | copy-done | bytes 32792
  5.2 54.0 %hss_sample.1 = (f32[4,4096]{1,0:T(4,128)S(1)}, f32[16,1024]{1,0:T(8,128)S(1)}, f32[1,8]{1,0:T(1,128)S(1)}, f32[1,2]{1,0:T(1,128)S(1)}) custom-call(bf16[4096,1024]{1,0:T(8,128)(2,1)} %a_hbm.1, bf16[128,128]{1,0:T(8,128)(2,1)S(1)} %copy-done.2, bf16[128,128]{1,0:T(8,128)(2,1)S(1)} %copy-done.3, bf16[4096,384]{1,0:T(8,128)(2,1)S(1)} %copy-done, ...), custom_call_target="tpu_custom_call" | custom-call | tf_op jit(solution)/shard_map/hss_sample/pallas_call | solution.py:479
  59.1 0.6 %copy.13 = f32[4,4096]{1,0:T(4,128)} copy(f32[4,4096]{1,0:T(4,128)S(1)} %get-tuple-element.16) | data formatting | bytes 131072
  59.8 0.6 %copy.14 = f32[16,1024]{1,0:T(8,128)} copy(f32[16,1024]{1,0:T(8,128)S(1)} %get-tuple-element.17) | data formatting | bytes 131072
  60.4 0.5 copy.15
  60.9 0.5 copy.16
Async XLA Ops:
  0.6 1.9 %copy-start = (bf16[4096,384]{1,0:T(8,128)(2,1)S(1)}, bf16[4096,384]{1,0:T(8,128)(2,1)}, u32[]{:S(2)}) copy-start(bf16[4096,384]{1,0:T(8,128)(2,1)} %rb_hbm.1) | copy-start | bytes 9437188
  2.5 1.1 %copy-start.1 = (bf16[1024,384]{1,0:T(8,128)(2,1)S(1)}, bf16[1024,384]{1,0:T(8,128)(2,1)}, u32[]{:S(2)}) copy-start(bf16[1024,384]{1,0:T(8,128)(2,1)} %cb_hbm.1) | copy-start | bytes 2359300
  3.7 0.8 %copy-start.2 = (bf16[128,128]{1,0:T(8,128)(2,1)S(1)}, bf16[128,128]{1,0:T(8,128)(2,1)}, u32[]{:S(2)}) copy-start(bf16[128,128]{1,0:T(8,128)(2,1)} %r_hbm.1) | copy-start | bytes 98308
  4.4 0.8 %copy-start.3 = (bf16[128,128]{1,0:T(8,128)(2,1)S(1)}, bf16[128,128]{1,0:T(8,128)(2,1)}, u32[]{:S(2)}) copy-start(bf16[128,128]{1,0:T(8,128)(2,1)} %l_hbm.1) | copy-start | bytes 98308

commit v2 on v1

v2 whole, which is shorter than its diff:
```python
import functools

import jax
import jax.numpy as jnp
from jax import lax
from jax.experimental import pallas as pl
from jax.experimental.pallas import tpu as pltpu
from jax.sharding import PartitionSpec as P

F32 = jnp.float32
BF16 = jnp.bfloat16
MESH = pl.DeviceIdType.MESH
NODE = 512
EARLIER = 384
SAMPLES = 128
NZ = 8
ROWS = 4096
COLS = 1024
QS = 4
VMEM_LIMIT = 67043328


def three_parts(value):
    hi = value.astype(BF16).astype(F32)
    rest = value - hi
    mid = rest.astype(BF16).astype(F32)
    low = rest - mid
    return jnp.concatenate([hi, mid, low], axis=0).astype(BF16)


def joined(stacked, count):
    return stacked[:count] + stacked[count : 2 * count] + stacked[2 * count :]


def parts_dot(value, other, contract):
    out = lax.dot_general(
        three_parts(value), other, (((1,), (contract,)), ((), ())), preferred_element_type=F32
    )
    return joined(out, value.shape[0])


def kernel(
    a_hbm, r_hbm, l_hbm, rb_hbm, cb_hbm,
    row_hbm, col_hbm, rs_hbm, cs_hbm,
    row_out, col_out, rs_out, cs_out,
    a_v, rg, r_raw, l_raw, lg, rb_v, rbt, cb_v, rowacc, cacc, cr, cr4, sx, srecv, tb,
    ra_aug, ra_fin, rb_fin, vrow, vrow_all, vcol, vcol_all,
    in_sem, out_sem, a_sem,
    r_ss, r_rs, la_ss, la_rs, lb_ss, lb_rs, lp_ss, lp_rs,
    d_ss, d_rs, sa_ss, sa_rs, sb_ss, sb_rs, c_ss, c_rs,
    vr_ss, vr_rs, vc_ss, vc_rs,
):
    z = lax.axis_index("row")
    c = lax.axis_index("col")
    core = lax.rem(c, 2)
    other = 1 - core
    x = lax.rem(lax.div(c, 2), 4)
    y = lax.div(c, 8)
    a0 = core * y + other * x
    b0 = core * x + other * y
    stride_a = 2 + 6 * core
    stride_b = 8 - 6 * core

    def za(step):
        return lax.rem(z + step + NZ, NZ)

    def at_a(step):
        return lax.rem(a0 + step + 4, 4)

    def at_b(step):
        return lax.rem(b0 + step + 4, 4)

    def dev_a(step):
        return (z, at_a(step) * stride_a + b0 * stride_b + core)

    def dev_b(step):
        return (z, a0 * stride_a + at_b(step) * stride_b + core)

    def dev_z(step):
        return (za(step), c)

    partner = (z, c + 1 - 2 * core)

    def remote(src, dst, ssem, rsem, device):
        return pltpu.make_async_remote_copy(
            src_ref=src, dst_ref=dst, send_sem=ssem, recv_sem=rsem,
            device_id=device, device_id_type=MESH,
        )

    sent = []

    def send(copy):
        copy.start()
        sent.append(copy)

    r_in = pltpu.make_async_copy(r_hbm, r_raw, in_sem.at[0])
    l_in = pltpu.make_async_copy(l_hbm, l_raw, in_sem.at[1])
    r_in.start()
    l_in.start()
    barrier = pltpu.get_barrier_semaphore()
    peers = [dev_z(1), dev_z(-1), dev_a(1), dev_a(-1), dev_b(1), dev_b(-1), partner]
    for peer in peers:
        pl.semaphore_signal(barrier, inc=1, device_id=peer, device_id_type=MESH)
    l_in.wait()
    own_u = a0 * 4 + b0
    lg[core, own_u] = l_raw[...].T
    r_in.wait()
    rg[z] = r_raw[...].T
    rb_in = pltpu.make_async_copy(rb_hbm, rb_v, in_sem.at[2])
    cb_in = pltpu.make_async_copy(cb_hbm, cb_v, in_sem.at[3])
    rb_in.start()
    a_in = []
    for part in range(8):
        rows = pl.ds(part * NODE, NODE)
        copy = pltpu.make_async_copy(a_hbm.at[rows], a_v.at[rows], a_sem.at[part])
        copy.start()
        a_in.append(copy)
    cb_in.start()
    pl.semaphore_wait(barrier, len(peers))

    def r_copy(side, kind):
        d = 1 if side == 0 else -1
        block = za((0, -d, -d, -3 * d)[kind])
        reach = (d, d, 2 * d, d)[kind]
        ref = rg.at[block] if kind < 3 else rg.at[block, pl.ds(64 * side, 64)]
        return remote(ref, ref, r_ss.at[side, kind], r_rs.at[side, kind], dev_z(reach))

    def l_slot(ra, rb):
        return at_a(ra) * 4 + at_b(rb)

    def la_full(side):
        d = 1 if side == 0 else -1
        ref = lg.at[core, own_u]
        return remote(ref, ref, la_ss.at[0, side], la_rs.at[0, side], dev_a(d))

    def la_half(side):
        d = 1 if side == 0 else -1
        ref = lg.at[core, l_slot(-d, 0), pl.ds(64 * side, 64)]
        return remote(ref, ref, la_ss.at[1, side], la_rs.at[1, side], dev_a(d))

    def lb_full(ra, side):
        d = 1 if side == 0 else -1
        ref = lg.at[core, l_slot(ra, 0)]
        return remote(ref, ref, lb_ss.at[0, ra, side], lb_rs.at[0, ra, side], dev_b(d))

    def lb_two(ra):
        ref = lg.at[core, l_slot(ra, 0)]
        return remote(ref, ref, lb_ss.at[1, ra, 0], lb_rs.at[1, ra, 0], dev_b(2))

    def lp(ra, rb):
        ref = lg.at[core, l_slot(ra, rb)]
        return remote(ref, ref, lp_ss.at[ra, rb], lp_rs.at[ra, rb], partner)

    def lb_arrived(ra):
        for side in (0, 1):
            lb_full(ra, side).wait_recv()
            send(lp(ra, 3 if side == 0 else 1))

    def lb_two_arrived(ra):
        lb_two(ra).wait_recv()
        send(lp(ra, 2))

    def row_term(node, blocks, left):
        rows = pl.ds(pl.multiple_of(node * NODE, NODE), NODE)
        right = jnp.concatenate(
            [a_v[rows, pl.ds(pl.multiple_of(k * 128, 128), 128)] for k in blocks], axis=1
        )
        return lax.dot_general(
            left, right, (((1,), (1,)), ((), ())), preferred_element_type=F32
        )

    def row_pass(blocks):
        left = jnp.concatenate([rg[k] for k in blocks], axis=1)

        def body(part, carry):
            for node in (2 * part, 2 * part + 1):
                rowacc[node] = row_term(node, blocks, left)
            return carry

        lax.fori_loop(0, 4, body, 0)

    def col_pass(groups, first):
        lefts, starts = [], []
        for mine, ra in groups:
            if mine:
                cc, sa, sb, a_at = core, stride_a, stride_b, at_a(ra)
            else:
                cc, sa, sb = other, 2 + 6 * other, 8 - 6 * other
                a_at = lax.rem(b0 + ra, 4)
            for b in range(4):
                lefts.append(lg[cc, a_at * 4 + b])
                starts.append(pl.multiple_of((a_at * sa + b * sb + cc) * 128, 128))
        left = jnp.concatenate(lefts, axis=1)
        right = jnp.concatenate([a_v[pl.ds(s, 128), :] for s in starts], axis=0)
        term = jnp.dot(left, right, preferred_element_type=F32).reshape(NZ, 2, 8, COLS)
        if first:
            cacc[...] = term
        else:
            cacc[...] += term

    for side in (0, 1):
        send(r_copy(side, 0))
    for side in (0, 1):
        send(la_full(side))
        send(lb_full(0, side))
    send(lp(0, 0))

    for side in (0, 1):
        r_copy(side, 0).wait_recv()
        send(r_copy(side, 1))
    for side in (0, 1):
        send(r_copy(side, 2))
    for side in (0, 1):
        la_full(side).wait_recv()
        send(la_half(side))
        ra = 3 if side == 0 else 1
        send(lb_full(ra, 0))
        send(lb_full(ra, 1))
    lb_arrived(0)
    for ra in (1, 3, 0):
        send(lb_two(ra))
    send(lp(3, 0))
    send(lp(1, 0))
    rb_in.wait()

    def turn(n, carry):
        rows = pl.ds(pl.multiple_of(n * NODE, NODE), NODE)
        rbt[n] = rb_v[rows, :].T
        return carry

    lax.fori_loop(0, 8, turn, 0)

    for side in (0, 1):
        la_half(side).wait_recv()
    send(lb_full(2, 0))
    send(lb_full(2, 1))
    send(lb_two(2))
    send(lp(2, 0))
    for side in (0, 1):
        r_copy(side, 1).wait_recv()
        r_copy(side, 2).wait_recv()
        send(r_copy(side, 3))
    lb_arrived(1)
    lb_arrived(3)
    for ra in (0, 1, 3):
        lb_two_arrived(ra)
    for copy in a_in:
        copy.wait()
    row_pass([za(k) for k in (1, -1, 2, -2, 3, -3)])
    col_pass([(True, 0), (True, 1), (True, 3)], True)

    lb_arrived(2)
    lb_two_arrived(2)
    for side in (0, 1):
        r_copy(side, 3).wait_recv()

    last = [z, za(4)]
    left = jnp.concatenate([rg[k] for k in last], axis=1)
    sub = lax.broadcasted_iota(jnp.int32, (8, NODE), 0)

    def d_copy(q):
        return remote(sx.at[other, q], srecv.at[q], d_ss.at[q], d_rs.at[q], partner)

    for q in range(QS):
        for nn in (0, 1):
            total = rowacc[2 * q + nn] + row_term(2 * q + nn, last, left)
            v = total.reshape(16, 8, NODE)
            w = pltpu.roll(v, 4, 1)
            for one in range(4):
                for bp in (0, 1):
                    t0, t1 = 8 * bp + one, 8 * bp + 4 + one
                    sx[0, q, nn, one, bp] = jnp.where(sub < 4, v[t0], w[t1])
                    t0 = 4 * one + 2 * bp
                    sx[1, q, nn, one, bp] = jnp.where(sub < 4, w[t0], v[t0 + 1])
        send(d_copy(q))

    def c_copy(side, kind, n):
        d = 1 if side == 0 else -1
        lanes = pl.ds(n * NODE, NODE)
        if kind == 0:
            src, dst = cacc.at[za(4), side, :, lanes], cr4.at[side, n]
        else:
            src = cacc.at[za((0, 3 * d, d, 2 * d)[kind]), :, :, lanes]
            dst = cr.at[kind - 1, side, n]
        reach = (2 * d, d, d, 2 * d)[kind]
        return remote(
            src, dst, c_ss.at[kind, side, n], c_rs.at[kind, side, n], dev_z(reach)
        )

    def sa_copy(kind, q, side):
        d = 1 if side == 0 else -1
        if kind == 0:
            src = sx.at[core, q, side, at_a(2)]
            dst = ra_aug.at[side, q]
        else:
            half = 1 - side if kind == 1 else side
            src = sx.at[core, q, half, at_a(d)]
            dst = ra_fin.at[side, q, half]
        return remote(src, dst, sa_ss.at[kind, q, side], sa_rs.at[kind, q, side], dev_a(d))

    def sb_copy(q, step):
        return remote(
            tb.at[q, at_b(step)], rb_fin.at[step, q],
            sb_ss.at[step, q], sb_rs.at[step, q], dev_b(step),
        )

    def chip_sum(q):
        d_copy(q).wait_recv()
        full = [(sx[core, q, nn] + srecv[q, nn]).reshape(64, NODE) for nn in (0, 1)]
        coeffs = [
            parts_dot(full[nn], rb_v[pl.ds((2 * q + nn) * NODE, NODE), :], 0) for nn in (0, 1)
        ]
        cleaned = [full[nn] - parts_dot(coeffs[nn], rbt[2 * q + nn], 0) for nn in (0, 1)]
        for nn in (0, 1):
            sx[core, q, nn] = cleaned[nn].reshape(4, 2, 8, NODE)
        for kind in (0, 1):
            for side in (0, 1):
                send(sa_copy(kind, q, side))

    def a_added(q):
        for side in (0, 1):
            d = 1 if side == 0 else -1
            sa_copy(0, q, side).wait_recv()
            sx[core, q, side, at_a(d)] += ra_aug[side, q]
            send(sa_copy(2, q, side))

    def a_summed(q):
        for kind in (1, 2):
            for side in (0, 1):
                sa_copy(kind, q, side).wait_recv()
        low = sx[core, q, 0, a0] + ra_fin[0, q, 0] + ra_fin[1, q, 0]
        high = sx[core, q, 1, a0] + ra_fin[0, q, 1] + ra_fin[1, q, 1]
        low_rolled, high_rolled = pltpu.roll(low, 4, 1), pltpu.roll(high, 4, 1)
        for bp in (0, 1):
            tb[q, 2 * bp] = jnp.where(sub < 4, low[bp], high_rolled[bp])
            tb[q, 2 * bp + 1] = jnp.where(sub < 4, low_rolled[bp], high[bp])
        for step in (1, 3, 2):
            send(sb_copy(q, step))

    for ra in range(4):
        for rb in range(4):
            lp(ra, rb).wait_recv()
    col_pass([(True, 2), (False, 0), (False, 1), (False, 3), (False, 2)], False)

    for n in (0, 1):
        for kind in (0, 1):
            for side in (0, 1):
                send(c_copy(side, kind, n))
    for n in (0, 1):
        for side in (0, 1):
            send(c_copy(side, 2, n))

    def c_added(n):
        lanes = pl.ds(n * NODE, NODE)
        for side in (0, 1):
            two = za(2 if side == 0 else -2)
            c_copy(side, 0, n).wait_recv()
            c_copy(side, 1, n).wait_recv()
            cacc[two, :, :, lanes] += cr[0, side, n]
            cacc[two, side, :, lanes] += cr4[side, n]
            send(c_copy(side, 3, n))

    chip_sum(0)
    chip_sum(1)
    chip_sum(2)
    chip_sum(3)
    a_added(0)
    c_added(0)
    a_added(1)
    c_added(1)
    a_added(2)
    a_added(3)
    a_summed(0)
    a_summed(1)
    a_summed(2)
    a_summed(3)

    lane8 = lax.broadcasted_iota(jnp.int32, (8, 128), 1)
    sub8 = lax.broadcasted_iota(jnp.int32, (8, 128), 0)
    cb_in.wait()
    col_sq = jnp.zeros((8, 128), F32)
    for n in (0, 1):
        lanes = pl.ds(n * NODE, NODE)
        for side in (0, 1):
            for kind in (2, 3):
                c_copy(side, kind, n).wait_recv()
        full = cacc[z, :, :, lanes] + cr[1, 0, n] + cr[1, 1, n] + cr[2, 0, n] + cr[2, 1, n]
        full = full.reshape(16, NODE)
        basis = cb_v[pl.ds(n * NODE, NODE), :]
        cleaned = full - parts_dot(parts_dot(full, basis, 0), basis, 1)
        col_out[:, lanes] = cleaned
        sq = jnp.sum(cleaned * cleaned, axis=1, keepdims=True)
        col_sq = col_sq + jnp.where(lane8 == n, sq[:8] + sq[8:], 0.0)
    vcol[...] = jnp.sum(col_sq, axis=0, keepdims=True)
    stores = [
        pltpu.make_async_copy(src, dst, out_sem.at[k])
        for k, (src, dst) in enumerate(
            [(row_out, row_hbm), (col_out, col_hbm), (rs_out, rs_hbm), (cs_out, cs_hbm)]
        )
    ]

    def vc_copy(j):
        return remote(vcol, vcol_all.at[j], vc_ss.at[j], vc_rs.at[j], dev_z(j))

    def vr_copy(j):
        return remote(
            vrow, vrow_all.at[j], vr_ss.at[j], vr_rs.at[j], (z, lax.rem(c + j, 32))
        )

    def loop(first, last, what):
        def body(j, carry):
            what(j)
            return carry

        lax.fori_loop(first, last, body, 0)

    loop(1, NZ, lambda j: vc_copy(j).start())
    stores[1].start()

    row_sq = jnp.zeros((8, 128), F32)
    for q in range(QS):
        for step in (1, 3, 2):
            sb_copy(q, step).wait_recv()
        cleaned = tb[q, b0] + rb_fin[1, q] + rb_fin[3, q] + rb_fin[2, q]
        row_out[:, pl.ds(2 * q * NODE, NODE)] = cleaned[:4]
        row_out[:, pl.ds((2 * q + 1) * NODE, NODE)] = cleaned[4:]
        sq = jnp.sum(cleaned * cleaned, axis=1, keepdims=True)
        place = jnp.where(sub8 < 4, 2 * q, 2 * q + 1)
        row_sq = row_sq + jnp.where(lane8 == place, sq, 0.0)
    vrow[...] = jnp.sum(row_sq, axis=0, keepdims=True)
    loop(1, 32, lambda j: vr_copy(j).start())
    stores[0].start()

    loop(1, NZ, lambda j: vc_copy(j).wait_recv())
    col_total = vcol[...]
    for j in range(1, NZ):
        col_total = col_total + vcol_all[j]
    scale = 1.0 / (SAMPLES * NODE)
    cs_out[...] = jnp.sqrt(col_total * scale)[:, :2]
    stores[3].start()

    for copy in sent:
        copy.wait_send()
    loop(1, NZ, lambda j: vc_copy(j).wait_send())

    loop(1, 32, lambda j: vr_copy(j).wait_recv())
    row_total = vrow[...]
    for j in range(1, 32):
        row_total = row_total + vrow_all[j]
    rs_out[...] = jnp.sqrt(row_total * scale)[:, :8]
    stores[2].start()
    loop(1, 32, lambda j: vr_copy(j).wait_send())
    for copy in stores:
        copy.wait()


def store_kernel(*refs):
    given, stored, held, sem = refs[:4], refs[4:8], refs[8:12], refs[12]
    loads = [pltpu.make_async_copy(given[k], held[k], sem.at[0, k]) for k in range(4)]
    stores = [pltpu.make_async_copy(held[k], stored[k], sem.at[1, k]) for k in range(4)]
    for copy in loads:
        copy.start()
    for load, store in zip(loads, stores):
        load.wait()
        store.start()
    for copy in stores:
        copy.wait()


def shards(front_matrix, right_random, left_random, row_basis, column_basis):
    vmem = pltpu.VMEM
    dma = pltpu.SemaphoreType.DMA
    row, col, rs, cs = pl.pallas_call(
        kernel,
        out_shape=(
            jax.ShapeDtypeStruct((4, ROWS), F32),
            jax.ShapeDtypeStruct((16, COLS), F32),
            jax.ShapeDtypeStruct((1, 8), F32),
            jax.ShapeDtypeStruct((1, 2), F32),
        ),
        in_specs=[pl.BlockSpec(memory_space=pltpu.HBM)] * 5,
        out_specs=[pl.BlockSpec(memory_space=pltpu.HBM)] * 4,
        scratch_shapes=[
            vmem((4, ROWS), F32), vmem((16, COLS), F32), vmem((1, 8), F32), vmem((1, 2), F32),
            vmem((ROWS, COLS), BF16),
            vmem((NZ, 128, 128), BF16),
            vmem((128, 128), BF16),
            vmem((128, 128), BF16),
            vmem((2, 16, 128, 128), BF16),
            vmem((ROWS, EARLIER), BF16),
            vmem((8, EARLIER, NODE), BF16),
            vmem((COLS, EARLIER), BF16),
            vmem((8, 128, NODE), F32),
            vmem((NZ, 2, 8, COLS), F32),
            vmem((3, 2, 2, 2, 8, NODE), F32),
            vmem((2, 2, 8, NODE), F32),
            vmem((2, QS, 2, 4, 2, 8, NODE), F32),
            vmem((QS, 2, 4, 2, 8, NODE), F32),
            vmem((QS, 4, 8, NODE), F32),
            vmem((2, QS, 2, 8, NODE), F32),
            vmem((2, QS, 2, 2, 8, NODE), F32),
            vmem((4, QS, 8, NODE), F32),
            vmem((1, 128), F32),
            vmem((32, 1, 128), F32),
            vmem((1, 128), F32),
            vmem((NZ, 1, 128), F32),
            dma((4,)), dma((4,)), dma((8,)),
            dma((2, 4)), dma((2, 4)),
            dma((2, 2)), dma((2, 2)),
            dma((2, 4, 2)), dma((2, 4, 2)),
            dma((4, 4)), dma((4, 4)),
            dma((QS,)), dma((QS,)),
            dma((3, QS, 2)), dma((3, QS, 2)),
            dma((4, QS)), dma((4, QS)),
            dma((4, 2, 2)), dma((4, 2, 2)),
            dma((32,)), dma((32,)),
            dma((NZ,)), dma((NZ,)),
        ],
        compiler_params=pltpu.CompilerParams(
            collective_id=0, has_side_effects=True, vmem_limit_bytes=VMEM_LIMIT
        ),
        name="hss_sample",
    )(front_matrix, right_random, left_random, row_basis, column_basis)
    results = (row, col, rs, cs)
    row, col, rs, cs = pl.pallas_call(
        store_kernel,
        out_shape=tuple(jax.ShapeDtypeStruct(v.shape, F32) for v in results),
        in_specs=[pl.BlockSpec(memory_space=pltpu.HBM)] * 4,
        out_specs=[pl.BlockSpec(memory_space=pltpu.HBM)] * 4,
        scratch_shapes=[vmem(v.shape, F32) for v in results] + [dma((2, 4))],
        compiler_params=pltpu.CompilerParams(vmem_limit_bytes=VMEM_LIMIT),
        name="store_results",
    )(*results)
    return row, col, rs.reshape(8), cs.reshape(2)


def solution(mesh):
    return jax.shard_map(
        shards,
        mesh=mesh,
        in_specs=(
            P("row", "col"), P(("col", "row"), None), P(("row", "col"), None),
            P("row", None), P("col", None),
        ),
        out_specs=(P("col", "row"), P("row", "col"), P("row"), P("col")),
        check_vma=False,
    )
```

time: 61.7 us -> 47.4 us (0.77)
  Pallas kernels: 54 us -> 46.5 us
  local copies, waits for them, and re-layouts: 6.81 us -> 0 us
    pallas_call x1, Pallas kernels: 54 us -> 45 us  [shards(): pl.pallas_call(kernel, out_shape=(jax.ShapeDtypeStruct((4, ROWS), F32), j...]
    unnamed x12 -> x0, local copies, waits for them, and re-layouts: 6.81 us -> none
    pallas_call x0 -> x1, Pallas kernels: none -> 1.57 us  [shards(): pl.pallas_call(store_kernel, out_shape=tuple((jax.ShapeDtypeStruct(v.shap...]
where the time goes in v2:
time: 47.4 us; the launch traced here: 47.2 us
  Pallas kernels  46.5 us (98%)
  between operations  0.64 us (1%)
    pallas_call x1, Pallas kernels, shards(): pl.pallas_call(kernel, out_shape=(jax.ShapeDtypeStruct((4, ROWS), F32), j...  45 us
    pallas_call x1, Pallas kernels, shards(): pl.pallas_call(store_kernel, out_shape=tuple((jax.ShapeDtypeStruct(v.shap...  1.57 us

profile of v2, /device:TPU:1, one launch (start us, length us, event | category | flops | bytes accessed | tf_op | source)
XLA Modules:
  0.0 47.2 jit_solution(15977044717597240018)
XLA Ops:
  0.6 45.0 %hss_sample.1 = (f32[4,4096]{1,0:T(4,128)}, f32[16,1024]{1,0:T(8,128)}, f32[1,8]{1,0:T(1,128)}, f32[1,2]{1,0:T(1,128)}) custom-call(bf16[4096,1024]{1,0:T(8,128)(2,1)} %a_hbm.1, bf16[128,128]{1,0:T(8,128)(2,1)} %r_hbm.1, bf16[128,128]{1,0:T(8,128)(2,1)} %l_hbm.1, bf16[4096,384]{1,0:T(8,128)(2,1)} %rb_hbm.1, bf16[1024,384]{1,0:T(8,128)(2,1)} %cb_hbm.1), custom_call_target="tpu_custom_call" | custom-call | tf_op jit(solution)/shard_map/hss_sample/pallas_call | solution.py:473
  45.6 1.6 %store_results.1 = (f32[4,4096]{1,0:T(4,128)}, f32[16,1024]{1,0:T(8,128)}, f32[1,8]{1,0:T(1,128)}, f32[1,2]{1,0:T(1,128)}) custom-call(f32[4,4096]{1,0:T(4,128)} %get-tuple-element.12.refs_0_, f32[16,1024]{1,0:T(8,128)} %get-tuple-element.13.refs_1_, f32[1,8]{1,0:T(1,128)} %get-tuple-element.14.refs_2_, f32[1,2]{1,0:T(1,128)} %get-tuple-element.15.refs_3_), custom_call_target="tpu_custom_call" | custom-call | tf_op jit(solution)/shard_map/store_results/pallas_call | solution.py:525

commit v3 on v2

--- a/solution.py
+++ b/solution.py
@@ -44,7 +44,7 @@
     row_hbm, col_hbm, rs_hbm, cs_hbm,
     row_out, col_out, rs_out, cs_out,
     a_v, rg, r_raw, l_raw, lg, rb_v, rbt, cb_v, rowacc, cacc, cr, cr4, sx, srecv, tb,
-    ra_aug, ra_fin, rb_fin, vrow, vrow_all, vcol, vcol_all,
+    ra_fin, rb_fin, vrow, vrow_all, vcol, vcol_all,
     in_sem, out_sem, a_sem,
     r_ss, r_rs, la_ss, la_rs, lb_ss, lb_rs, lp_ss, lp_rs,
     d_ss, d_rs, sa_ss, sa_rs, sb_ss, sb_rs, c_ss, c_rs,
@@ -169,12 +169,16 @@
             left, right, (((1,), (1,)), ((), ())), preferred_element_type=F32
         )
 
-    def row_pass(blocks):
+    def row_pass(blocks, first):
         left = jnp.concatenate([rg[k] for k in blocks], axis=1)
 
         def body(part, carry):
             for node in (2 * part, 2 * part + 1):
-                rowacc[node] = row_term(node, blocks, left)
+                term = row_term(node, blocks, left)
+                if first:
+                    rowacc[node] = term
+                else:
+                    rowacc[node] += term
             return carry
 
         lax.fori_loop(0, 4, body, 0)
@@ -229,6 +233,9 @@
         return carry
 
     lax.fori_loop(0, 8, turn, 0)
+    for copy in a_in:
+        copy.wait()
+    row_pass([z, za(1), za(-1)], True)
 
     for side in (0, 1):
         la_half(side).wait_recv()
@@ -244,9 +251,7 @@
     lb_arrived(3)
     for ra in (0, 1, 3):
         lb_two_arrived(ra)
-    for copy in a_in:
-        copy.wait()
-    row_pass([za(k) for k in (1, -1, 2, -2, 3, -3)])
+    row_pass([za(k) for k in (2, -2, 3, -3)], False)
     col_pass([(True, 0), (True, 1), (True, 3)], True)
 
     lb_arrived(2)
@@ -254,7 +259,7 @@
     for side in (0, 1):
         r_copy(side, 3).wait_recv()
 
-    last = [z, za(4)]
+    last = [za(4)]
     left = jnp.concatenate([rg[k] for k in last], axis=1)
     sub = lax.broadcasted_iota(jnp.int32, (8, NODE), 0)
 
@@ -287,16 +292,11 @@
             src, dst, c_ss.at[kind, side, n], c_rs.at[kind, side, n], dev_z(reach)
         )
 
-    def sa_copy(kind, q, side):
-        d = 1 if side == 0 else -1
-        if kind == 0:
-            src = sx.at[core, q, side, at_a(2)]
-            dst = ra_aug.at[side, q]
-        else:
-            half = 1 - side if kind == 1 else side
-            src = sx.at[core, q, half, at_a(d)]
-            dst = ra_fin.at[side, q, half]
-        return remote(src, dst, sa_ss.at[kind, q, side], sa_rs.at[kind, q, side], dev_a(d))
+    def sa_copy(q, step):
+        return remote(
+            sx.at[core, q, :, at_a(step)], ra_fin.at[step, q],
+            sa_ss.at[step, q], sa_rs.at[step, q], dev_a(step),
+        )
 
     def sb_copy(q, step):
         return remote(
@@ -313,29 +313,24 @@
         cleaned = [full[nn] - parts_dot(coeffs[nn], rbt[2 * q + nn], 0) for nn in (0, 1)]
         for nn in (0, 1):
             sx[core, q, nn] = cleaned[nn].reshape(4, 2, 8, NODE)
-        for kind in (0, 1):
-            for side in (0, 1):
-                send(sa_copy(kind, q, side))
-
-    def a_added(q):
-        for side in (0, 1):
-            d = 1 if side == 0 else -1
-            sa_copy(0, q, side).wait_recv()
-            sx[core, q, side, at_a(d)] += ra_aug[side, q]
-            send(sa_copy(2, q, side))
+        for step in (2, 1, 3):
+            send(sa_copy(q, step))
 
     def a_summed(q):
-        for kind in (1, 2):
-            for side in (0, 1):
-                sa_copy(kind, q, side).wait_recv()
-        low = sx[core, q, 0, a0] + ra_fin[0, q, 0] + ra_fin[1, q, 0]
-        high = sx[core, q, 1, a0] + ra_fin[0, q, 1] + ra_fin[1, q, 1]
+        for step in (1, 3, 2):
+            sa_copy(q, step).wait_recv()
+        low, high = [
+            sx[core, q, nn, a0] + ra_fin[1, q, nn] + ra_fin[3, q, nn] + ra_fin[2, q, nn]
+            for nn in (0, 1)
+        ]
         low_rolled, high_rolled = pltpu.roll(low, 4, 1), pltpu.roll(high, 4, 1)
         for bp in (0, 1):
             tb[q, 2 * bp] = jnp.where(sub < 4, low[bp], high_rolled[bp])
             tb[q, 2 * bp + 1] = jnp.where(sub < 4, low_rolled[bp], high[bp])
         for step in (1, 3, 2):
             send(sb_copy(q, step))
+
+    chip_sum(0)
 
     for ra in range(4):
         for rb in range(4):
@@ -360,18 +355,13 @@
             cacc[two, side, :, lanes] += cr4[side, n]
             send(c_copy(side, 3, n))
 
-    chip_sum(0)
     chip_sum(1)
     chip_sum(2)
     chip_sum(3)
-    a_added(0)
+    a_summed(0)
     c_added(0)
-    a_added(1)
+    a_summed(1)
     c_added(1)
-    a_added(2)
-    a_added(3)
-    a_summed(0)
-    a_summed(1)
     a_summed(2)
     a_summed(3)
 
@@ -497,8 +487,7 @@
             vmem((2, QS, 2, 4, 2, 8, NODE), F32),
             vmem((QS, 2, 4, 2, 8, NODE), F32),
             vmem((QS, 4, 8, NODE), F32),
-            vmem((2, QS, 2, 8, NODE), F32),
-            vmem((2, QS, 2, 2, 8, NODE), F32),
+            vmem((4, QS, 2, 2, 8, NODE), F32),
             vmem((4, QS, 8, NODE), F32),
             vmem((1, 128), F32),
             vmem((32, 1, 128), F32),
@@ -510,7 +499,7 @@
             dma((2, 4, 2)), dma((2, 4, 2)),
             dma((4, 4)), dma((4, 4)),
             dma((QS,)), dma((QS,)),
-            dma((3, QS, 2)), dma((3, QS, 2)),
+            dma((4, QS)), dma((4, QS)),
             dma((4, QS)), dma((4, QS)),
             dma((4, 2, 2)), dma((4, 2, 2)),
             dma((32,)), dma((32,)),

time: 47.4 us -> 45.1 us (0.951)
  Pallas kernels: 46.5 us -> 44.3 us
    pallas_call x1, Pallas kernels: 45 us -> 42.7 us  [shards(): pl.pallas_call(kernel, out_shape=(jax.ShapeDtypeStruct((4, ROWS), F32), j...]
where the time goes in v3:
time: 45.1 us; the launch traced here: 44.9 us
  Pallas kernels  44.3 us (98%)
  between operations  0.64 us (1%)
    pallas_call x1, Pallas kernels, shards(): pl.pallas_call(kernel, out_shape=(jax.ShapeDtypeStruct((4, ROWS), F32), j...  42.7 us
    pallas_call x1, Pallas kernels, shards(): pl.pallas_call(store_kernel, out_shape=tuple((jax.ShapeDtypeStruct(v.shap...  1.57 us

profile of v3, /device:TPU:1, one launch (start us, length us, event | category | flops | bytes accessed | tf_op | source)
XLA Modules:
  0.0 44.9 jit_solution(7068726023096287436)
XLA Ops:
  0.6 42.7 %hss_sample.1 = (f32[4,4096]{1,0:T(4,128)}, f32[16,1024]{1,0:T(8,128)}, f32[1,8]{1,0:T(1,128)}, f32[1,2]{1,0:T(1,128)}) custom-call(bf16[4096,1024]{1,0:T(8,128)(2,1)} %a_hbm.1, bf16[128,128]{1,0:T(8,128)(2,1)} %r_hbm.1, bf16[128,128]{1,0:T(8,128)(2,1)} %l_hbm.1, bf16[4096,384]{1,0:T(8,128)(2,1)} %rb_hbm.1, bf16[1024,384]{1,0:T(8,128)(2,1)} %cb_hbm.1), custom_call_target="tpu_custom_call" | custom-call | tf_op jit(solution)/shard_map/hss_sample/pallas_call | solution.py:463
  43.3 1.6 %store_results.1 = (f32[4,4096]{1,0:T(4,128)}, f32[16,1024]{1,0:T(8,128)}, f32[1,8]{1,0:T(1,128)}, f32[1,2]{1,0:T(1,128)}) custom-call(f32[4,4096]{1,0:T(4,128)} %get-tuple-element.12.refs_0_, f32[16,1024]{1,0:T(8,128)} %get-tuple-element.13.refs_1_, f32[1,8]{1,0:T(1,128)} %get-tuple-element.14.refs_2_, f32[1,2]{1,0:T(1,128)} %get-tuple-element.15.refs_3_), custom_call_target="tpu_custom_call" | custom-call | tf_op jit(solution)/shard_map/store_results/pallas_call | solution.py:514
